TPU v7x, 32 devices: a whole 2x2x4 slice. The times are simulated.
32 devices in a mesh: band: 16 (over z, x, core), ga: 2 (over y).
Axes of the slice: x: 2, y: 2, z: 4, core: 2. Of those that a mesh axis runs over, the one named last changes fastest.
Arguments:
- psi: float32 [2, 4096, 65536], P(None, 'band', 'ga'), may hold values from -0.0234375 to 0.0234375
- hx: float32 [2, 256, 65536], P(None, 'band', 'ga'), may hold values from -6 to 6
Outputs:
- h_sub: float32 [2, 4096, 256], P(None, ('band', 'ga'))
All inputs are finite; a program needn't handle non-finite values.
Results may differ from a plain program's by a relative error of at most 0.00007.
Values sent between devices are 32-bit elements; how exact they have to be, the bound alone decides.
A program may use at most 192 MiB of HBM per device.

v0:
```python
import jax
import jax.numpy as jnp
from jax import lax
from jax.sharding import PartitionSpec as P

SHARES = (22, 10)


def contract(left, right):
    return lax.dot_general(
        left,
        right,
        (((1,), (1,)), ((), ())),
        precision=lax.Precision.HIGH,
        preferred_element_type=jnp.float32,
    )


def per_device(psi, hx):
    parts, rows, depth = psi.shape
    unit = depth // sum(SHARES)
    bands = psi.reshape(parts * rows, depth)
    total = None
    first = 0
    pieces = []
    for share in SHARES:
        last = first + share * unit
        piece = lax.all_gather(hx[:, :, first:last], "band", axis=1, tiled=True)
        pieces.append((first, last, piece))
        first = last
    for first, last, piece in pieces:
        product = contract(bands[:, first:last], piece.reshape(-1, last - first))
        total = product if total is None else total + product
    vectors = total.shape[1] // parts
    real_left, imag_left = (total[:rows], total[rows:])
    real_tile = real_left[:, :vectors] + imag_left[:, vectors:]
    imag_tile = real_left[:, vectors:] - imag_left[:, :vectors]
    partial_value = jnp.stack([real_tile, imag_tile], axis=0)
    n = lax.axis_size("ga")
    me = lax.axis_index("ga")
    height = rows // n

    def block(owner):
        return lax.dynamic_slice_in_dim(partial_value, owner * height, height, axis=1)

    result = block(me)
    for step in range(1, n):
        ring = [(i, (i + step) % n) for i in range(n)]
        result = result + lax.ppermute(block(lax.rem(me + step, n)), "ga", ring)
    return result


def solution(mesh):
    in_specs = (P(None, "band", "ga"), P(None, "band", "ga"))
    out_specs = P(None, ("band", "ga"), None)
    return jax.shard_map(
        per_device, mesh=mesh, in_specs=in_specs, out_specs=out_specs, check_vma=False
    )
```

profile of v0, /device:TPU:0, one launch (start us, length us, event | category | flops | bytes accessed | tf_op | source)
XLA Modules:
  0.0 389.9 jit_solution(5589482113664164910)
XLA Ops:
  6.5 0.0 all-gather.3.cloned.1.call-start
  6.5 3.6 slice.31
  10.1 0.0 all-gather.3.cloned.1.call-update
  10.2 0.0 all-gather.5.cloned.1.call-start
  10.2 2.5 slice.33
  12.7 0.0 all-gather.5.cloned.1.call-update
  12.7 227.6 %all-gather.3.cloned.1.call-done = f32[2,256,22528]{2,1,0:T(8,128)} async-done(((f32[2,16,22528]{2,1,0:T(8,128)}), f32[2,256,22528]{2,1,0:T(8,128)}) %all-gather.3.cloned.1.call-update) | async-done | bytes 46137360 | tf_op jit(solution)/shard_map/all_gather | solution.py:28
  240.3 43.3 %fusion = f32[512,512]{1,0:T(8,128)S(1)} fusion(f32[512,22528]{1,0:T(8,128)} %bitcast.9, f32[512,32768]{1,0:T(8,128)} %bitcast), kind=kOutput, calls=%fused_computation | convolution fusion | flops 35433480192 | bytes 93323264 | tf_op jit(solution)/shard_map/dot_general | solution.py:10
  283.6 67.1 %all-gather.5.cloned.1.call-done = f32[2,256,10240]{2,1,0:T(8,128)} async-done(((f32[2,16,10240]{2,1,0:T(8,128)}), f32[2,256,10240]{2,1,0:T(8,128)}) %all-gather.5.cloned.1.call-update) | async-done | bytes 20971536 | tf_op jit(solution)/shard_map/all_gather | solution.py:28
  350.7 22.9 %fusion.4 = f32[512,512]{1,0:T(8,128)S(1)} fusion(f32[512,512]{1,0:T(8,128)S(1)} %fusion, f32[512,10240]{1,0:T(8,128)} %bitcast.10, f32[512,32768]{1,0:T(8,128)} %bitcast), kind=kOutput, calls=%fused_computation.4 | convolution fusion | flops 16106389504 | bytes 44040192 | tf_op jit(solution)/shard_map/dot_general | solution.py:10
  373.6 0.1 fusion.10
  373.8 1.5 collective-permute-start
  375.3 7.0 %collective-permute-done = f32[2,128,256]{2,1,0:T(8,128)S(1)} collective-permute-done((f32[2,128,256]{2,1,0:T(8,128)S(1)}, f32[2,128,256]{2,1,0:T(8,128)S(1)}, u32[]{:S(2)}, u32[]{:S(2)}) %collective-permute-start) | collective-permute-done | bytes 262176 | tf_op jit(solution)/shard_map/ppermute | solution.py:49
  382.3 0.7 fusion.9
  (1 shorter events, 0.0 us)
Async XLA Ops:
  6.5 233.8 %all-gather.3.cloned.1.call-start = ((), (), s32[]{:S(2)}) async-start(), calls=%async_computation | async-start | bytes 49020928 | tf_op jit(solution)/shard_map/all_gather | solution.py:28
  10.2 340.5 %all-gather.5.cloned.1.call-start = ((), (), s32[]{:S(2)}) async-start(), calls=%async_computation.1 | async-start | bytes 22282240 | tf_op jit(solution)/shard_map/all_gather | solution.py:28
  373.8 8.5 %collective-permute-start = (f32[2,128,256]{2,1,0:T(8,128)S(1)}, f32[2,128,256]{2,1,0:T(8,128)S(1)}, u32[]{:S(2)}, u32[]{:S(2)}) collective-permute-start(f32[2,128,256]{2,1,0:T(8,128)S(1)} %fusion.7), channel_id=1, source_target_pairs={{0,1},{1,0},{2,3},{3,2},{4,5},{5,4},{6,7},{7,6},{8,9},{9,8},{10,11... | collective-permute-start | bytes 786440 | tf_op jit(solution)/shard_map/ppermute | solution.py:49
Sparse Core Ops, SparseCore 0:
  10.3 230.0 all-gather.2
  241.9 108.7 all-gather.4
where the time goes:
time: 390 us
  waiting for transfers between devices  302 us (77%)
  matrix products  66.2 us (17%)
  between operations  13.4 us (3%)
  local copies, waits for them, and re-layouts  6.08 us (2%)
    all_gather x2, waiting for transfers between devices, per_device(): piece = lax.all_gather(hx[:, :, first:last], 'band', axis=1, tiled=True)  295 us
    dot_general x2, matrix products, contract(): lax.dot_general(left, right, (((1,), (1,)), ((), ())), precision=lax.Prec...  66.2 us
  transfers between devices with their start and end apart: 3, of which 3 were waited for; matrix products, arithmetic and copies ran while one was open for 12% of the time, Pallas kernels for 0%

commit v1 on v0

--- a/solution.py
+++ b/solution.py
@@ -25,7 +25,7 @@
     pieces = []
     for share in SHARES:
         last = first + share * unit
-        piece = lax.all_gather(hx[:, :, first:last], "band", axis=1, tiled=True)
+        piece = jnp.concatenate(lax.all_gather(hx[:, :, first:last], "band"), axis=1)
         pieces.append((first, last, piece))
         first = last
     for first, last, piece in pieces:

time: 390 us -> 466 us (1.19)
  local copies, waits for them, and re-layouts: 6.08 us -> 55.7 us
  waiting for transfers between devices: 302 us -> 327 us
    reshape x0 -> x2, local copies, waits for them, and re-layouts: none -> 49.6 us  [per_device(): jnp.concatenate(lax.all_gather(hx[:, :, first:last], 'band'), axis=1)]
    all_gather x2, waiting for transfers between devices: 295 us -> 320 us  [per_device(): lax.all_gather(hx[:, :, first:last], 'band')]
  transfers between devices with their start and end apart: 3 -> 3, of which waited for: 3 -> 3; matrix products, arithmetic and copies ran while one was open for 12% -> 4% of each run, Pallas kernels for 0% -> 0%
where the time goes in v1:
time: 466 us
  waiting for transfers between devices  327 us (70%)
  matrix products  66.5 us (14%)
  local copies, waits for them, and re-layouts  55.7 us (12%)
  between operations  13.4 us (3%)
    all_gather x2, waiting for transfers between devices, per_device(): lax.all_gather(hx[:, :, first:last], 'band')  320 us
    dot_general x2, matrix products, contract(): lax.dot_general(left, right, (((1,), (1,)), ((), ())), precision=lax.Prec...  66.5 us
    reshape x2, local copies, waits for them, and re-layouts, per_device(): jnp.concatenate(lax.all_gather(hx[:, :, first:last], 'band'), axis=1)  49.6 us
  transfers between devices with their start and end apart: 3, of which 3 were waited for; matrix products, arithmetic and copies ran while one was open for 4% of the time, Pallas kernels for 0%

profile of v1, /device:TPU:0, one launch (start us, length us, event | category | flops | bytes accessed | tf_op | source)
XLA Modules:
  0.0 465.5 jit_solution(13488049225596107915)
XLA Ops:
  6.5 0.0 all-gather.7.cloned.1.call-start
  6.5 2.5 slice.33
  9.0 0.0 all-gather.7.cloned.1.call-update
  9.0 0.0 all-gather.5.cloned.1.call-start
  9.1 3.6 slice.31
  12.7 0.0 all-gather.5.cloned.1.call-update
  12.7 108.0 %all-gather.7.cloned.1.call-done = f32[32,16,10240]{2,1,0:T(8,128)} async-done(((f32[2,16,10240]{2,1,0:T(8,128)}), f32[32,16,10240]{2,1,0:T(8,128)}) %all-gather.7.cloned.1.call-update) | async-done | bytes 20971536 | tf_op jit(solution)/shard_map/all_gather | solution.py:28
  120.7 16.4 %copy.6 = f32[2,16,16,10240]{3,2,1,0:T(8,128)} copy(f32[2,16,16,10240]{3,2,0,1:T(8,128)} %bitcast.18) | data formatting | bytes 41943040 | tf_op jit(solution)/shard_map/reshape | solution.py:28
  137.1 212.5 %all-gather.5.cloned.1.call-done = f32[32,16,22528]{2,1,0:T(8,128)} async-done(((f32[2,16,22528]{2,1,0:T(8,128)}), f32[32,16,22528]{2,1,0:T(8,128)}) %all-gather.5.cloned.1.call-update) | async-done | bytes 46137360 | tf_op jit(solution)/shard_map/all_gather | solution.py:28
  349.6 33.2 %copy.5 = f32[2,16,16,22528]{3,2,1,0:T(8,128)} copy(f32[2,16,16,22528]{3,2,0,1:T(8,128)} %bitcast.17) | data formatting | bytes 92274688 | tf_op jit(solution)/shard_map/reshape | solution.py:28
  382.8 43.3 %fusion = f32[512,512]{1,0:T(8,128)S(1)} fusion(f32[512,22528]{1,0:T(8,128)} %bitcast.15, f32[512,32768]{1,0:T(8,128)} %bitcast), kind=kOutput, calls=%fused_computation | convolution fusion | flops 35433480192 | bytes 93323264 | tf_op jit(solution)/shard_map/dot_general | solution.py:10
  426.2 23.1 %fusion.4 = f32[512,512]{1,0:T(8,128)S(1)} fusion(f32[512,512]{1,0:T(8,128)S(1)} %fusion, f32[512,10240]{1,0:T(8,128)} %bitcast.16, f32[512,32768]{1,0:T(8,128)} %bitcast), kind=kOutput, calls=%fused_computation.4 | convolution fusion | flops 16106389504 | bytes 44040192 | tf_op jit(solution)/shard_map/dot_general | solution.py:10
  449.3 0.1 fusion.10
  449.4 1.5 collective-permute-start
  451.0 7.0 %collective-permute-done = f32[2,128,256]{2,1,0:T(8,128)S(1)} collective-permute-done((f32[2,128,256]{2,1,0:T(8,128)S(1)}, f32[2,128,256]{2,1,0:T(8,128)S(1)}, u32[]{:S(2)}, u32[]{:S(2)}) %collective-permute-start) | collective-permute-done | bytes 262176 | tf_op jit(solution)/shard_map/ppermute | solution.py:49
  458.0 0.7 fusion.9
  (1 shorter events, 0.0 us)
Async XLA Ops:
  6.5 114.2 %all-gather.7.cloned.1.call-start = ((), (), s32[]{:S(2)}) async-start(), calls=%async_computation.1 | async-start | bytes 22282240 | tf_op jit(solution)/shard_map/all_gather | solution.py:28
  9.0 340.6 %all-gather.5.cloned.1.call-start = ((), (), s32[]{:S(2)}) async-start(), calls=%async_computation | async-start | bytes 49020928 | tf_op jit(solution)/shard_map/all_gather | solution.py:28
  449.4 8.5 %collective-permute-start = (f32[2,128,256]{2,1,0:T(8,128)S(1)}, f32[2,128,256]{2,1,0:T(8,128)S(1)}, u32[]{:S(2)}, u32[]{:S(2)}) collective-permute-start(f32[2,128,256]{2,1,0:T(8,128)S(1)} %fusion.7), channel_id=1, source_target_pairs={{0,1},{1,0},{2,3},{3,2},{4,5},{5,4},{6,7},{7,6},{8,9},{9,8},{10,11... | collective-permute-start | bytes 786440 | tf_op jit(solution)/shard_map/ppermute | solution.py:49
Sparse Core Ops, SparseCore 0:
  9.2 111.4 all-gather.6
  122.3 227.2 all-gather.4
